TPU v7x, 256 devices: a whole 4x4x8 slice. The times are simulated.
256 devices in a mesh: row: 8 (over z_lo, y), col: 32 (over z_hi, x, core).
Axes of the slice: x: 4, y: 4, z: 8 (z_hi: 4, z_lo: 2; z = z_hi * 2 + z_lo), core: 2. Of those that a mesh axis runs over, the one named last changes fastest.
Arguments:
- alignment: float32 [512, 768, 256], P('row', 'col'), may hold values from -40 to 40
- seq_mask: int32 [512], replicated, may hold values 0 or 1
- res_mask: int32 [768], replicated, may hold values 0 or 1
- attn_gain: float32 [256], replicated, may hold values from 0.5 to 1.5
- outer_product_gain: float32 [256], replicated, may hold values from 0.5 to 1.5
- w_query: bfloat16 [256, 256], replicated, may hold values from -24 to 24
- w_key: bfloat16 [256, 256], replicated, may hold values from -2 to 2
- w_value: bfloat16 [256, 256], replicated, may hold values from -0.375 to 0.375
- w_gate: bfloat16 [256, 256], replicated, may hold values from -0.375 to 0.375
- output_weight: bfloat16 [256, 256], replicated, may hold values from -0.375 to 0.375
- w_left: bfloat16 [256, 32], replicated, may hold values from -0.375 to 0.375
- w_right: bfloat16 [256, 32], replicated, may hold values from -0.375 to 0.375
- w_pair: bfloat16 [1024, 128], replicated, may hold values from -3 to 3
Outputs:
- alignment_output: float32 [512, 768, 256], P('row', 'col')
- pair_increment: float32 [768, 768, 128], P('row', 'col')
All inputs are finite; a program needn't handle non-finite values.
Results may differ from a plain program's by a relative error of at most 0.0095.
Values may be sent and summed in bfloat16 or wider, within the bound.
No kernel may reach another device: no remote copies, remote signals or barrier semaphores. Data moves between devices by JAX's collectives and lax.ppermute only.
A program may use at most 128 MiB of HBM per device.

v0:
```python
import jax
import jax.numpy as jnp
from jax import lax
from jax.sharding import PartitionSpec as P

HEADS = 8
HEAD_DIM = 32


def sent_to_all(shard, axis):
    copies = jnp.broadcast_to(shard, (lax.axis_size(axis), *shard.shape))
    return lax.all_to_all(copies, axis, split_axis=0, concat_axis=0, tiled=True)


def laid_out(blocks, dim):
    blocks = jnp.moveaxis(blocks, 0, dim)
    shape = blocks.shape
    return blocks.reshape(*shape[:dim], shape[dim] * shape[dim + 1], *shape[dim + 2 :])


def gathered_copies(shard, axis, dim):
    blocks = sent_to_all(shard, axis)
    return laid_out(blocks, dim)


def normalized_rows(values, gains):
    average = jnp.mean(values, -1, keepdims=True)
    centred = values - average
    spread = jnp.mean(centred * centred, -1, keepdims=True)
    return centred * lax.rsqrt(spread + 1e-05) * gains


def shards(
    alignment,
    seq_mask,
    res_mask,
    attn_gain,
    outer_product_gain,
    w_query,
    w_key,
    w_value,
    w_gate,
    output_weight,
    w_left,
    w_right,
    w_pair,
):
    seq_dev, res_dev, channel_width = alignment.shape
    row_count = lax.axis_size("row")
    col_count = lax.axis_size("col")
    sequence_total = seq_mask.shape[0]
    hidden = w_query.shape[1]
    query_scale = HEAD_DIM ** (-0.5)
    key_bias = jnp.where(seq_mask > 0, 0.0, -1000000000.0).astype(jnp.float32)
    normed = normalized_rows(alignment, attn_gain).astype(jnp.bfloat16)
    normed = normed.reshape(seq_dev, row_count, res_dev // row_count, channel_width)

    def column(column_parts):
        col_query, col_key, col_value, col_gate = column_parts
        heads_query = col_query.reshape(sequence_total, HEADS, HEAD_DIM)
        heads_key = col_key.reshape(sequence_total, HEADS, HEAD_DIM)
        heads_value = col_value.reshape(sequence_total, HEADS, HEAD_DIM)
        logits = (
            jnp.einsum("shd,thd->hst", heads_query, heads_key, preferred_element_type=jnp.float32)
            + key_bias[None, None, :]
        )
        weights = jax.nn.softmax(logits, axis=-1).astype(jnp.bfloat16)
        attended = jnp.einsum(
            "hst,thd->shd", weights, heads_value, preferred_element_type=jnp.float32
        ).reshape(sequence_total, hidden)
        return (jax.nn.sigmoid(col_gate) * attended).astype(jnp.bfloat16)

    tokens = lax.all_to_all(normed, "row", split_axis=1, concat_axis=0, tiled=True)[:, 0]
    residues = tokens.shape[1]
    token_rows = tokens.reshape(-1, channel_width)
    queries = (
        jnp.dot(token_rows, w_query, preferred_element_type=jnp.float32) * query_scale
    ).astype(jnp.bfloat16)
    key_rows = jnp.dot(token_rows, w_key, preferred_element_type=jnp.float32).astype(jnp.bfloat16)
    value_rows = jnp.dot(token_rows, w_value, preferred_element_type=jnp.float32).astype(
        jnp.bfloat16
    )
    gate_lin = jnp.dot(token_rows, w_gate, preferred_element_type=jnp.float32)

    def arrange(values):
        return values.reshape(sequence_total, residues, -1).transpose(1, 0, 2)

    gated_output = lax.map(
        column, (arrange(queries), arrange(key_rows), arrange(value_rows), arrange(gate_lin))
    )
    gated_output = gated_output.transpose(1, 0, 2)[:, None]
    returned_value = lax.all_to_all(gated_output, "row", split_axis=0, concat_axis=1, tiled=True)
    returned_value = returned_value.reshape(-1, hidden)
    alignment_output = alignment + jnp.dot(
        returned_value, output_weight, preferred_element_type=jnp.float32
    ).reshape(seq_dev, res_dev, channel_width)
    row_index = lax.axis_index("row")
    col_index = lax.axis_index("col")
    side_width = w_left.shape[1]
    second_normalized = (
        normalized_rows(alignment_output, outer_product_gain)
        .astype(jnp.bfloat16)
        .reshape(-1, channel_width)
    )
    own_seq = lax.dynamic_slice_in_dim(seq_mask, row_index * seq_dev, seq_dev, 0)
    own_res = lax.dynamic_slice_in_dim(res_mask, col_index * res_dev, res_dev, 0)
    side_mask = (own_seq[:, None] * own_res[None, :]).astype(jnp.float32)[:, :, None]
    left = (
        (
            jnp.dot(second_normalized, w_left, preferred_element_type=jnp.float32).reshape(
                seq_dev, res_dev, side_width
            )
            * side_mask
        )
        .astype(jnp.bfloat16)
        .reshape(seq_dev, -1)
    )
    right = (
        (
            jnp.dot(second_normalized, w_right, preferred_element_type=jnp.float32).reshape(
                seq_dev, res_dev, side_width
            )
            * side_mask
        )
        .astype(jnp.bfloat16)
        .reshape(seq_dev, -1)
    )
    pair_rows = res_dev * col_count // row_count
    contraction = (((0,), (0,)), ((), ()))
    right_all = gathered_copies(right, "row", 0)
    group = seq_dev // col_count
    right_order = (
        right_all.reshape(row_count, col_count, group, -1)
        .transpose(1, 0, 2, 3)
        .reshape(sequence_total, -1)
    )
    spread_out = lax.all_to_all(left, "col", split_axis=0, concat_axis=1, tiled=True)
    own_block = lax.all_to_all(spread_out, "row", split_axis=1, concat_axis=0, tiled=True)
    products = lax.dot_general(
        lax.all_gather(own_block, "col", axis=0, tiled=True),
        right_order,
        contraction,
        preferred_element_type=jnp.float32,
    )
    outer_sum = (
        products.reshape(pair_rows, side_width, res_dev, side_width)
        .transpose(0, 2, 1, 3)
        .reshape(-1, side_width * side_width)
        .astype(jnp.bfloat16)
    )
    projected_output = jnp.dot(outer_sum, w_pair, preferred_element_type=jnp.float32).reshape(
        pair_rows, res_dev, -1
    )
    pair_res = lax.dynamic_slice_in_dim(res_mask, row_index * pair_rows, pair_rows, 0)
    live_total = jnp.sum(seq_mask)
    count_values = jnp.maximum(live_total * pair_res[:, None] * own_res[None, :], 1).astype(
        jnp.float32
    )
    return (alignment_output, projected_output / count_values[:, :, None])


def solution(mesh):
    in_specs = (P("row", "col", None), P(), P(), P(), P(), P(), P(), P(), P(), P(), P(), P(), P())
    out_specs = (P("row", "col", None), P("row", "col", None))
    return jax.shard_map(shards, mesh=mesh, in_specs=in_specs, out_specs=out_specs, check_vma=False)
```

profile of v0, /device:TPU:5, one launch (start us, length us, event | category | flops | bytes accessed | tf_op | source)
XLA Modules:
  0.0 247.4 jit_solution(861617664489180695)
XLA Ops:
  11.4 5.5 %all-to-all-start = ((bf16[64,8,3,256]{3,0,2,1:T(8,128)(2,1)}), bf16[64,8,3,256]{3,0,2,1:T(8,128)(2,1)S(1)}, u32[]{:S(2)}, u32[]{:S(2)}) async-start(bf16[64,8,3,256]{3,0,2,1:T(8,128)(2,1)} %bitcast.5), calls=%async_computation | async-start | bytes 1572864 | tf_op jit(solution)/shard_map/all_to_all | solution.py:73
  17.0 11.5 %all-to-all-done = bf16[64,8,3,256]{3,0,2,1:T(8,128)(2,1)S(1)} async-done(((bf16[64,8,3,256]{3,0,2,1:T(8,128)(2,1)}), bf16[64,8,3,256]{3,0,2,1:T(8,128)(2,1)S(1)}, u32[]{:S(2)}, u32[]{:S(2)}) %all-to-all-start) | async-done | bytes 786464 | tf_op jit(solution)/shard_map/all_to_all | solution.py:73
  31.1 2.4 reshape_squeeze.3
  42.5 2.5 reshape.159
  46.6 2.6 %convolution_bitcast_fusion = f32[3,512,256]{2,1,0:T(8,128)} fusion(bf16[512,3,256]{2,0,1:T(8,128)(2,1)} %bitcast.103, bf16[256,256]{1,0:T(8,128)(2,1)S(1)} %copy-done.3), kind=kOutput, calls=%fused_computation.25 | convolution fusion | flops 201326592 | bytes 2490368 | tf_op jit(solution)/shard_map/dot_general | solution.py:83
  49.2 40.3 %while.10 = (s32[]{:T(128)}, bf16[3,512,256]{1,2,0:T(8,128)(2,1)}, f32[3,512,256]{2,1,0:T(8,128)}, bf16[3,512,256]{1,2,0:T(8,128)(2,1)}, bf16[3,512,256]{1,2,0:T...) while((s32[]{:T(128)}, bf16[3,512,256]{1,2,0:T(8,128)(2,1)}, ...), condition=%wide.region_5.6_spmd, body=%wide.region_2.5_spmd.sunk | while | flops 279577088 | bytes 23104096 | solution.py:88
  50.3 5.0 %fusion.43 = (f32[8,512]{1,0:T(8,128)S(1)}, f32[8,512,512]{1,2,0:T(8,128)}) fusion(f32[512]{0:T(512)S(1)} %get-tuple-element.174, bf16[512,8,32]{0,2,1:T(8,128)(2,1)S(1)} %bitcast.97, bf16[512,8,32]{0,2,1:T(8,128)(2,1)S(1)} %bitcast.96), kind=kOutput, calls=%fused_computation.46.clone.1 | convolution fusion | flops 140509696 | bytes 8931328 | tf_op jit(solution)/shard_map/while/body/eval_jaxpr/sub | solution.py:67
  56.3 4.2 %fusion.44 = f32[8,32,512]{2,1,0:T(8,128)S(1)} fusion(bf16[512,8,32]{0,2,1:T(8,128)(2,1)S(1)} %bitcast.95, f32[8,512,512]{1,2,0:T(8,128)} %get-tuple-element.150, f32[8,512]{1,0:T(8,128)S(1)} %get-tuple-element.151), kind=kOutput, calls=%fused_computation.6.clone.1 | convolution fusion | flops 138412032 | bytes 9191424 | tf_op jit(solution)/shard_map/while/body/eval_jaxpr/hst,thd->shd/dot_general | solution.py:68
  63.7 5.0 %fusion.43 = (f32[8,512]{1,0:T(8,128)S(1)}, f32[8,512,512]{1,2,0:T(8,128)}) fusion(f32[512]{0:T(512)S(1)} %get-tuple-element.174, bf16[512,8,32]{0,2,1:T(8,128)(2,1)S(1)} %bitcast.97, bf16[512,8,32]{0,2,1:T(8,128)(2,1)S(1)} %bitcast.96), kind=kOutput, calls=%fused_computation.46.clone.1 | convolution fusion | flops 140509696 | bytes 8931328 | tf_op jit(solution)/shard_map/while/body/eval_jaxpr/sub | solution.py:67
  69.7 4.2 %fusion.44 = f32[8,32,512]{2,1,0:T(8,128)S(1)} fusion(bf16[512,8,32]{0,2,1:T(8,128)(2,1)S(1)} %bitcast.95, f32[8,512,512]{1,2,0:T(8,128)} %get-tuple-element.150, f32[8,512]{1,0:T(8,128)S(1)} %get-tuple-element.151), kind=kOutput, calls=%fused_computation.6.clone.1 | convolution fusion | flops 138412032 | bytes 9191424 | tf_op jit(solution)/shard_map/while/body/eval_jaxpr/hst,thd->shd/dot_general | solution.py:68
  77.1 5.0 %fusion.43 = (f32[8,512]{1,0:T(8,128)S(1)}, f32[8,512,512]{1,2,0:T(8,128)}) fusion(f32[512]{0:T(512)S(1)} %get-tuple-element.174, bf16[512,8,32]{0,2,1:T(8,128)(2,1)S(1)} %bitcast.97, bf16[512,8,32]{0,2,1:T(8,128)(2,1)S(1)} %bitcast.96), kind=kOutput, calls=%fused_computation.46.clone.1 | convolution fusion | flops 140509696 | bytes 8931328 | tf_op jit(solution)/shard_map/while/body/eval_jaxpr/sub | solution.py:67
  83.1 4.2 %fusion.44 = f32[8,32,512]{2,1,0:T(8,128)S(1)} fusion(bf16[512,8,32]{0,2,1:T(8,128)(2,1)S(1)} %bitcast.95, f32[8,512,512]{1,2,0:T(8,128)} %get-tuple-element.150, f32[8,512]{1,0:T(8,128)S(1)} %get-tuple-element.151), kind=kOutput, calls=%fused_computation.6.clone.1 | convolution fusion | flops 138412032 | bytes 9191424 | tf_op jit(solution)/shard_map/while/body/eval_jaxpr/hst,thd->shd/dot_general | solution.py:68
  89.5 2.3 copy.104
  91.8 4.3 %all-to-all-start.1 = ((bf16[512,1,3,256]{3,2,1,0:T(4,128)(2,1)}), bf16[512,1,3,256]{3,2,1,0:T(4,128)(2,1)S(1)}, u32[]{:S(2)}, u32[]{:S(2)}) async-start(bf16[512,1,3,256]{3,2,1,0:T(4,128)(2,1)} %bitcast.102), calls=%async_computation.1 | async-start | bytes 2097152 | tf_op jit(solution)/shard_map/all_to_all | solution.py:92
  97.0 14.0 %all-to-all-done.1 = bf16[512,1,3,256]{3,2,1,0:T(4,128)(2,1)S(1)} async-done(((bf16[512,1,3,256]{3,2,1,0:T(4,128)(2,1)}), bf16[512,1,3,256]{3,2,1,0:T(4,128)(2,1)S(1)}, u32[]{:S(2)}, u32[]{:S(2)}) %all-to-all-start.1) | async-done | bytes 786464 | tf_op jit(solution)/shard_map/all_to_all | solution.py:92
  114.8 19.5 %all_to_all.70 = bf16[32,2,768]{2,1,0:T(2,128)(2,1)S(1)} all-to-all(bf16[32,2,768]{2,1,0:T(2,128)(2,1)S(1)} %all_to_all.57), channel_id=1, replica_groups=mesh['row'=8,'col'=32] {'col'}, dimensions={0} | all-to-all | bytes 196608 | tf_op jit(solution)/shard_map/all_to_all | solution.py:137
  134.3 8.1 %all_to_all.71 = bf16[2,8,3072]{2,0,1:T(2,128)(2,1)S(1)} all-to-all(bf16[2,8,3072]{2,0,1:T(2,128)(2,1)S(1)} %bitcast.112), channel_id=1, replica_groups=mesh['row'=8,'col'=32] {'row'}, dimensions={1} | all-to-all | bytes 196608 | tf_op jit(solution)/shard_map/all_to_all | solution.py:138
  145.3 3.5 %all-to-all-start.4 = ((bf16[8,64,768]{2,1,0:T(8,128)(2,1)}), bf16[8,64,768]{2,1,0:T(8,128)(2,1)S(1)}, u32[]{:S(2)}, u32[]{:S(2)}) async-start(bf16[8,64,768]{2,1,0:T(8,128)(2,1)} %broadcast_in_dim.23), calls=%async_computation.4 | async-start | bytes 1572864 | tf_op jit(solution)/shard_map/all_to_all | solution.py:12
  151.0 8.0 %all-to-all-done.4 = bf16[8,64,768]{2,1,0:T(8,128)(2,1)S(1)} async-done(((bf16[8,64,768]{2,1,0:T(8,128)(2,1)}), bf16[8,64,768]{2,1,0:T(8,128)(2,1)S(1)}, u32[]{:S(2)}, u32[]{:S(2)}) %all-to-all-start.4) | async-done | bytes 786464 | tf_op jit(solution)/shard_map/all_to_all | solution.py:12
  161.6 35.4 %all-gather.2.cloned.1.call-done = bf16[512,3072]{1,0:T(8,128)(2,1)} async-done(((bf16[16,3072]{1,0:T(8,128)(2,1)}), bf16[512,3072]{1,0:T(8,128)(2,1)}) %all-gather.2.cloned.1.call-update) | async-done | bytes 3145744 | tf_op jit(solution)/shard_map/all_gather | solution.py:140
  197.0 3.2 %copy.114 = bf16[3072,512]{1,0:T(8,128)(2,1)S(1)} copy(bf16[3072,512]{0,1:T(8,128)(2,1)} %bitcast.105) | data formatting | bytes 6291456 | tf_op jit(solution)/shard_map/dot_general | solution.py:139
  200.2 13.7 %convert_bitcast_fusion = bf16[96,24,32,32]{3,2,1,0:T(8,128)(2,1)} fusion(bf16[96,32,512,1]{2,1,3,0:T(8,128)(2,1)S(1)} %bitcast.106, bf16[24,32,512,1]{2,1,0,3:T(8,128)(2,1)} %bitcast.110), kind=kOutput, calls=%fused_computation.15 | convolution fusion | flops 2418278400 | bytes 8650752 | tf_op jit(solution)/shard_map/dot_general | solution.py:139
  213.9 20.1 %copy.120 = bf16[96,24,32,32]{0,3,2,1:T(8,128)(2,1)} copy(bf16[96,24,32,32]{3,2,1,0:T(8,128)(2,1)} %convert_bitcast_fusion) | data formatting | bytes 9437184 | tf_op jit(solution)/shard_map/convert_element_type | solution.py:149
  234.1 4.8 %convolution_divide_fusion = f32[96,24,128]{2,0,1:T(8,128)S(1)} fusion(bf16[96,24,1024]{0,2,1:T(8,128)(2,1)} %bitcast.98, f32[96,24]{0,1:T(8,128)S(1)} %maximum_convert_fusion, bf16[1024,128]{1,0:T(8,128)(2,1)S(1)} %copy-done), kind=kOutput, calls=%fused_computation.27 | convolution fusion | flops 604274688 | bytes 6169600 | tf_op jit(solution)/shard_map/dot_general | solution.py:151
  (89 shorter events, 43.7 us)
Async XLA Ops:
  7.2 226.9 %copy-start = (bf16[1024,128]{1,0:T(8,128)(2,1)S(1)}, bf16[1024,128]{1,0:T(8,128)(2,1)}, u32[]{:S(2)}) copy-start(bf16[1024,128]{1,0:T(8,128)(2,1)} %param.27) | copy-start | bytes 786436
  7.2 1.9 copy-start.1
  7.2 2.7 %copy-start.9 = (f32[256]{0:T(256)S(1)}, f32[256]{0:T(256)}, u32[]{:S(2)}) copy-start(f32[256]{0:T(256)} %param.18) | copy-start | bytes 3076
  9.9 7.0 %copy-start.8 = (s32[512]{0:T(512)S(1)}, s32[512]{0:T(512)}, u32[]{:S(2)}) copy-start(s32[512]{0:T(512)} %param.16) | copy-start | bytes 6148
  11.4 17.1 %all-to-all-start = ((bf16[64,8,3,256]{3,0,2,1:T(8,128)(2,1)}), bf16[64,8,3,256]{3,0,2,1:T(8,128)(2,1)S(1)}, u32[]{:S(2)}, u32[]{:S(2)}) async-start(bf16[64,8,3,256]{3,0,2,1:T(8,128)(2,1)} %bitcast.5), calls=%async_computation | async-start | bytes 1572864 | tf_op jit(solution)/shard_map/all_to_all | solution.py:73
  30.1 3.4 %copy-start.5 = (bf16[256,256]{1,0:T(8,128)(2,1)S(1)}, bf16[256,256]{1,0:T(8,128)(2,1)}, u32[]{:S(2)}) copy-start(bf16[256,256]{1,0:T(8,128)(2,1)} %param.22) | copy-start | bytes 393220
  33.9 3.5 %copy-start.6 = (bf16[256,256]{1,0:T(8,128)(2,1)S(1)}, bf16[256,256]{1,0:T(8,128)(2,1)}, u32[]{:S(2)}) copy-start(bf16[256,256]{1,0:T(8,128)(2,1)} %param.20) | copy-start | bytes 393220
  37.7 3.5 %copy-start.7 = (bf16[256,256]{1,0:T(8,128)(2,1)S(1)}, bf16[256,256]{1,0:T(8,128)(2,1)}, u32[]{:S(2)}) copy-start(bf16[256,256]{1,0:T(8,128)(2,1)} %param.21) | copy-start | bytes 393220
  42.5 4.1 %copy-start.3 = (bf16[256,256]{1,0:T(8,128)(2,1)S(1)}, bf16[256,256]{1,0:T(8,128)(2,1)}, u32[]{:S(2)}) copy-start(bf16[256,256]{1,0:T(8,128)(2,1)} %param.23) | copy-start | bytes 393220
  91.8 19.2 %all-to-all-start.1 = ((bf16[512,1,3,256]{3,2,1,0:T(4,128)(2,1)}), bf16[512,1,3,256]{3,2,1,0:T(4,128)(2,1)S(1)}, u32[]{:S(2)}, u32[]{:S(2)}) async-start(bf16[512,1,3,256]{3,2,1,0:T(4,128)(2,1)} %bitcast.102), calls=%async_computation.1 | async-start | bytes 2097152 | tf_op jit(solution)/shard_map/all_to_all | solution.py:92
  96.0 100.9 %all-gather.2.cloned.1.call-start = ((), (), s32[]{:S(2)}) async-start(), calls=%async_computation.5 | async-start | bytes 3244032 | tf_op jit(solution)/shard_map/all_gather | solution.py:140
  111.0 0.9 copy-start.4
  112.7 30.3 %copy-start.2 = (f32[64,24,256]{2,1,0:T(8,128)}, f32[64,24,256]{2,1,0:T(8,128)S(1)}, u32[]{:S(2)}) copy-start(f32[64,24,256]{2,1,0:T(8,128)S(1)} %get-tuple-element.100) | copy-start | bytes 4718596
  112.7 0.9 copy-start.10
  112.7 0.9 copy-start.12
  113.6 29.4 %copy-start.11 = (bf16[256,32]{0,1:T(8,128)(2,1)S(1)}, bf16[256,32]{0,1:T(8,128)(2,1)}, u32[]{:S(2)}) copy-start(bf16[256,32]{0,1:T(8,128)(2,1)} %param.26) | copy-start | bytes 49156
  145.3 13.7 %all-to-all-start.4 = ((bf16[8,64,768]{2,1,0:T(8,128)(2,1)}), bf16[8,64,768]{2,1,0:T(8,128)(2,1)S(1)}, u32[]{:S(2)}, u32[]{:S(2)}) async-start(bf16[8,64,768]{2,1,0:T(8,128)(2,1)} %broadcast_in_dim.23), calls=%async_computation.4 | async-start | bytes 1572864 | tf_op jit(solution)/shard_map/all_to_all | solution.py:12
Sparse Core Ops, SparseCore 0:
  143.2 53.7 all-gather.1
where the time goes:
time: 249 us; the launch traced here: 247 us
  waiting for transfers between devices  69 us (28%)
  local copies, waits for them, and re-layouts  60.3 us (24%)
  matrix products  53.5 us (21%)
  blocking collectives  27.5 us (11%)
  between operations  14.3 us (6%)
  starting transfers between devices  13.4 us (5%)
  other arithmetic  9.38 us (4%)
    all_gather x1, waiting for transfers between devices, shards(): lax.all_gather(own_block, 'col', axis=0, tiled=True)  35.4 us
    convert_element_type x1, local copies, waits for them, and re-layouts, shards(): outer_sum = products.reshape(pair_rows, side_width, res_dev, side_width)....  20.1 us
    all_to_all x1, blocking collectives, shards(): lax.all_to_all(left, 'col', split_axis=0, concat_axis=1, tiled=True)  19.5 us
    sub x3, matrix products, column(): weights = jax.nn.softmax(logits, axis=-1).astype(jnp.bfloat16)  15 us
    all_to_all x1, waiting for transfers between devices, shards(): lax.all_to_all(gated_output, 'row', split_axis=0, concat_axis=1, tiled=True)  14 us
    dot_general x1, matrix products, shards(): lax.dot_general(lax.all_gather(own_block, 'col', axis=0, tiled=True), rig...  13.7 us
    dot_general x3, matrix products, column(): jnp.einsum('hst,thd->shd', weights, heads_value, preferred_element_type=j...  12.7 us
    all_to_all x1, waiting for transfers between devices, shards(): lax.all_to_all(normed, 'row', split_axis=1, concat_axis=0, tiled=True)[:, 0]  11.5 us
  transfers between devices with their start and end apart: 4, of which 4 were waited for; matrix products, arithmetic and copies ran while one was open for 3% of the time, Pallas kernels for 0%

commit v1 on v0

--- a/solution.py
+++ b/solution.py
@@ -2,9 +2,18 @@
 import jax.numpy as jnp
 from jax import lax
 from jax.sharding import PartitionSpec as P
+from jax.lax import all_to_all, axis_size
 
 HEADS = 8
 HEAD_DIM = 32
+
+
+def fit_plate(field_in, d_out, at_axis):
+    mixed_arr = jnp.concatenate(
+        all_to_all(jnp.stack(jnp.split(field_in, axis_size("row"), axis=d_out)), "row", 0, 0),
+        axis=at_axis,
+    )
+    return mixed_arr
 
 
 def sent_to_all(shard, axis):
@@ -70,7 +79,7 @@
         ).reshape(sequence_total, hidden)
         return (jax.nn.sigmoid(col_gate) * attended).astype(jnp.bfloat16)
 
-    tokens = lax.all_to_all(normed, "row", split_axis=1, concat_axis=0, tiled=True)[:, 0]
+    tokens = fit_plate(normed, 1, 0)[:, 0]
     residues = tokens.shape[1]
     token_rows = tokens.reshape(-1, channel_width)
     queries = (

time: 249 us -> 261 us (1.048)
  local copies, waits for them, and re-layouts: 60.3 us -> 70.9 us
    reshape x3, local copies, waits for them, and re-layouts: 4.84 us -> 9.9 us  [arrange(): return values.reshape(sequence_total, residues, -1).transpose(1, 0, 2)]
    unnamed x27 -> x34, local copies, waits for them, and re-layouts: 2.5 us -> 7.02 us
where the time goes in v1:
time: 261 us; the launch traced here: 260 us
  local copies, waits for them, and re-layouts  70.9 us (27%)
  waiting for transfers between devices  69.9 us (27%)
  matrix products  54.9 us (21%)
  blocking collectives  27.6 us (11%)
  between operations  14.3 us (5%)
  starting transfers between devices  13.4 us (5%)
  other arithmetic  8.53 us (3%)
    all_gather x1, waiting for transfers between devices, shards(): lax.all_gather(own_block, 'col', axis=0, tiled=True)  36.3 us
    convert_element_type x1, local copies, waits for them, and re-layouts, shards(): outer_sum = products.reshape(pair_rows, side_width, res_dev, side_width)....  20.1 us
    all_to_all x1, blocking collectives, shards(): lax.all_to_all(left, 'col', split_axis=0, concat_axis=1, tiled=True)  19.6 us
    sub x3, matrix products, column(): weights = jax.nn.softmax(logits, axis=-1).astype(jnp.bfloat16)  15.1 us
    dot_general x1, matrix products, shards(): lax.dot_general(lax.all_gather(own_block, 'col', axis=0, tiled=True), rig...  14.5 us
    all_to_all x1, waiting for transfers between devices, shards(): lax.all_to_all(gated_output, 'row', split_axis=0, concat_axis=1, tiled=True)  14 us
    dot_general x3, matrix products, column(): jnp.einsum('hst,thd->shd', weights, heads_value, preferred_element_type=j...  12.7 us
    all_to_all x1, waiting for transfers between devices, fit_plate(): all_to_all(jnp.stack(jnp.split(field_in, axis_size('row'), axis=d_out)),...  11.5 us
  transfers between devices with their start and end apart: 4, of which 4 were waited for; matrix products, arithmetic and copies ran while one was open for 3% of the time, Pallas kernels for 0%

profile of v1, /device:TPU:5, one launch (start us, length us, event | category | flops | bytes accessed | tf_op | source)
XLA Modules:
  0.0 259.6 jit_solution(8009710530299399604)
XLA Ops:
  15.7 5.5 %all-to-all-start = ((bf16[8,64,1,3,256]{4,1,3,2,0:T(8,128)(2,1)}), bf16[8,64,1,3,256]{4,1,3,2,0:T(8,128)(2,1)S(1)}, u32[]{:S(2)}, u32[]{:S(2)}) async-start(bf16[8,64,1,3,256]{4,1,3,2,0:T(8,128)(2,1)} %fusion.16), calls=%async_computation | async-start | bytes 1572864 | tf_op jit(solution)/shard_map/all_to_all | solution.py:13
  21.3 11.5 %all-to-all-done = bf16[8,64,1,3,256]{4,1,3,2,0:T(8,128)(2,1)S(1)} async-done(((bf16[8,64,1,3,256]{4,1,3,2,0:T(8,128)(2,1)}), bf16[8,64,1,3,256]{4,1,3,2,0:T(8,128)(2,1)S(1)}, u32[]{:S(2)}, u32[]{:S(2)}) %all-to-all-start) | async-done | bytes 786464 | tf_op jit(solution)/shard_map/all_to_all | solution.py:13
  34.4 2.4 reshape_squeeze_reshape.3
  38.1 3.3 %reshape.156 = bf16[512,3,256]{2,1,0:T(4,128)(2,1)} reshape(bf16[1536,256]{1,0:T(8,128)(2,1)} %convolution_convert_fusion.1) | data formatting | bytes 1572864 | tf_op jit(solution)/shard_map/reshape | solution.py:95
  45.0 3.3 %reshape.157 = bf16[512,3,256]{2,1,0:T(4,128)(2,1)} reshape(bf16[1536,256]{1,0:T(8,128)(2,1)} %fusion.9) | data formatting | bytes 1572864 | tf_op jit(solution)/shard_map/reshape | solution.py:95
  51.8 3.3 %reshape.158 = bf16[512,3,256]{2,1,0:T(4,128)(2,1)} reshape(bf16[1536,256]{1,0:T(8,128)(2,1)} %convolution_convert_fusion) | data formatting | bytes 1572864 | tf_op jit(solution)/shard_map/reshape | solution.py:95
  59.0 40.3 %while.10 = (s32[]{:T(128)}, bf16[3,512,256]{1,2,0:T(8,128)(2,1)}, f32[3,512,256]{2,1,0:T(8,128)}, bf16[3,512,256]{1,2,0:T(8,128)(2,1)}, bf16[3,512,256]{1,2,0:T...) while((s32[]{:T(128)}, bf16[3,512,256]{1,2,0:T(8,128)(2,1)}, ...), condition=%wide.region_5.6_spmd, body=%wide.region_2.5_spmd.sunk | while | flops 279577088 | bytes 23104096 | solution.py:97
  60.0 5.0 %fusion.51 = (f32[8,512]{1,0:T(8,128)S(1)}, f32[8,512,512]{1,2,0:T(8,128)}) fusion(f32[512]{0:T(512)S(1)} %get-tuple-element.174, bf16[512,8,32]{0,2,1:T(8,128)(2,1)S(1)} %bitcast.124, bf16[512,8,32]{0,2,1:T(8,128)(2,1)S(1)} %bitcast.123), kind=kOutput, calls=%fused_computation.62.clone.1 | convolution fusion | flops 140509696 | bytes 8931328 | tf_op jit(solution)/shard_map/while/body/eval_jaxpr/sub | solution.py:76
  66.0 4.2 %fusion.52 = f32[8,32,512]{2,1,0:T(8,128)S(1)} fusion(bf16[512,8,32]{0,2,1:T(8,128)(2,1)S(1)} %bitcast.122, f32[8,512,512]{1,2,0:T(8,128)} %get-tuple-element.150, f32[8,512]{1,0:T(8,128)S(1)} %get-tuple-element.151), kind=kOutput, calls=%fused_computation.6.clone.1 | convolution fusion | flops 138412032 | bytes 9191424 | tf_op jit(solution)/shard_map/while/body/eval_jaxpr/hst,thd->shd/dot_general | solution.py:77
  73.5 5.0 %fusion.51 = (f32[8,512]{1,0:T(8,128)S(1)}, f32[8,512,512]{1,2,0:T(8,128)}) fusion(f32[512]{0:T(512)S(1)} %get-tuple-element.174, bf16[512,8,32]{0,2,1:T(8,128)(2,1)S(1)} %bitcast.124, bf16[512,8,32]{0,2,1:T(8,128)(2,1)S(1)} %bitcast.123), kind=kOutput, calls=%fused_computation.62.clone.1 | convolution fusion | flops 140509696 | bytes 8931328 | tf_op jit(solution)/shard_map/while/body/eval_jaxpr/sub | solution.py:76
  79.5 4.2 %fusion.52 = f32[8,32,512]{2,1,0:T(8,128)S(1)} fusion(bf16[512,8,32]{0,2,1:T(8,128)(2,1)S(1)} %bitcast.122, f32[8,512,512]{1,2,0:T(8,128)} %get-tuple-element.150, f32[8,512]{1,0:T(8,128)S(1)} %get-tuple-element.151), kind=kOutput, calls=%fused_computation.6.clone.1 | convolution fusion | flops 138412032 | bytes 9191424 | tf_op jit(solution)/shard_map/while/body/eval_jaxpr/hst,thd->shd/dot_general | solution.py:77
  86.9 5.0 %fusion.51 = (f32[8,512]{1,0:T(8,128)S(1)}, f32[8,512,512]{1,2,0:T(8,128)}) fusion(f32[512]{0:T(512)S(1)} %get-tuple-element.174, bf16[512,8,32]{0,2,1:T(8,128)(2,1)S(1)} %bitcast.124, bf16[512,8,32]{0,2,1:T(8,128)(2,1)S(1)} %bitcast.123), kind=kOutput, calls=%fused_computation.62.clone.1 | convolution fusion | flops 140509696 | bytes 8931328 | tf_op jit(solution)/shard_map/while/body/eval_jaxpr/sub | solution.py:76
  92.9 4.2 %fusion.52 = f32[8,32,512]{2,1,0:T(8,128)S(1)} fusion(bf16[512,8,32]{0,2,1:T(8,128)(2,1)S(1)} %bitcast.122, f32[8,512,512]{1,2,0:T(8,128)} %get-tuple-element.150, f32[8,512]{1,0:T(8,128)S(1)} %get-tuple-element.151), kind=kOutput, calls=%fused_computation.6.clone.1 | convolution fusion | flops 138412032 | bytes 9191424 | tf_op jit(solution)/shard_map/while/body/eval_jaxpr/hst,thd->shd/dot_general | solution.py:77
  101.6 4.3 %all-to-all-start.1 = ((bf16[512,1,3,256]{3,2,1,0:T(4,128)(2,1)}), bf16[512,1,3,256]{3,2,1,0:T(4,128)(2,1)S(1)}, u32[]{:S(2)}, u32[]{:S(2)}) async-start(bf16[512,1,3,256]{3,2,1,0:T(4,128)(2,1)} %bitcast.129), calls=%async_computation.1 | async-start | bytes 2097152 | tf_op jit(solution)/shard_map/all_to_all | solution.py:101
  106.8 14.0 %all-to-all-done.1 = bf16[512,1,3,256]{3,2,1,0:T(4,128)(2,1)S(1)} async-done(((bf16[512,1,3,256]{3,2,1,0:T(4,128)(2,1)}), bf16[512,1,3,256]{3,2,1,0:T(4,128)(2,1)S(1)}, u32[]{:S(2)}, u32[]{:S(2)}) %all-to-all-start.1) | async-done | bytes 786464 | tf_op jit(solution)/shard_map/all_to_all | solution.py:101
  124.7 19.6 %all_to_all.60 = bf16[32,2,768]{2,1,0:T(2,128)(2,1)S(1)} all-to-all(bf16[32,2,768]{2,1,0:T(2,128)(2,1)S(1)} %all_to_all.47), channel_id=1, replica_groups=mesh['row'=8,'col'=32] {'col'}, dimensions={0} | all-to-all | bytes 196608 | tf_op jit(solution)/shard_map/all_to_all | solution.py:146
  144.2 8.1 %all_to_all.61 = bf16[2,8,3072]{2,0,1:T(2,128)(2,1)S(1)} all-to-all(bf16[2,8,3072]{2,0,1:T(2,128)(2,1)S(1)} %bitcast.147), channel_id=1, replica_groups=mesh['row'=8,'col'=32] {'row'}, dimensions={1} | all-to-all | bytes 196608 | tf_op jit(solution)/shard_map/all_to_all | solution.py:147
  155.2 3.5 %all-to-all-start.4 = ((bf16[8,64,768]{2,1,0:T(8,128)(2,1)}), bf16[8,64,768]{2,1,0:T(8,128)(2,1)S(1)}, u32[]{:S(2)}, u32[]{:S(2)}) async-start(bf16[8,64,768]{2,1,0:T(8,128)(2,1)} %broadcast_in_dim.23), calls=%async_computation.4 | async-start | bytes 1572864 | tf_op jit(solution)/shard_map/all_to_all | solution.py:21
  161.0 8.0 %all-to-all-done.4 = bf16[8,64,768]{2,1,0:T(8,128)(2,1)S(1)} async-done(((bf16[8,64,768]{2,1,0:T(8,128)(2,1)}), bf16[8,64,768]{2,1,0:T(8,128)(2,1)S(1)}, u32[]{:S(2)}, u32[]{:S(2)}) %all-to-all-start.4) | async-done | bytes 786464 | tf_op jit(solution)/shard_map/all_to_all | solution.py:21
  170.6 36.3 %all-gather.2.cloned.1.call-done = bf16[512,3072]{1,0:T(8,128)(2,1)} async-done(((bf16[16,3072]{1,0:T(8,128)(2,1)}), bf16[512,3072]{1,0:T(8,128)(2,1)}) %all-gather.2.cloned.1.call-update) | async-done | bytes 3145744 | tf_op jit(solution)/shard_map/all_gather | solution.py:149
  206.9 4.7 %copy.121 = bf16[3072,512]{1,0:T(8,128)(2,1)} copy(bf16[3072,512]{0,1:T(8,128)(2,1)} %bitcast.132) | data formatting | bytes 6291456 | tf_op jit(solution)/shard_map/dot_general | solution.py:148
  211.6 14.5 %convert_bitcast_fusion = bf16[96,24,32,32]{3,2,1,0:T(8,128)(2,1)} fusion(bf16[96,32,512,1]{2,1,3,0:T(8,128)(2,1)} %bitcast.133, bf16[24,32,512,1]{2,1,0,3:T(8,128)(2,1)S(1)} %bitcast.145), kind=kOutput, calls=%fused_computation.15 | convolution fusion | flops 2418278400 | bytes 8650752 | tf_op jit(solution)/shard_map/dot_general | solution.py:148
  226.1 20.1 %copy.127 = bf16[96,24,32,32]{0,3,2,1:T(8,128)(2,1)} copy(bf16[96,24,32,32]{3,2,1,0:T(8,128)(2,1)} %convert_bitcast_fusion) | data formatting | bytes 9437184 | tf_op jit(solution)/shard_map/convert_element_type | solution.py:158
  246.3 4.8 %convolution_divide_fusion = f32[96,24,128]{2,0,1:T(8,128)S(1)} fusion(bf16[96,24,1024]{0,2,1:T(8,128)(2,1)} %bitcast.125, f32[96,24]{0,1:T(8,128)S(1)} %maximum_convert_fusion, bf16[1024,128]{1,0:T(8,128)(2,1)S(1)} %copy-done), kind=kOutput, calls=%fused_computation.27 | convolution fusion | flops 604274688 | bytes 6169600 | tf_op jit(solution)/shard_map/dot_general | solution.py:160
  (97 shorter events, 50.2 us)
Async XLA Ops:
  7.2 239.1 %copy-start = (bf16[1024,128]{1,0:T(8,128)(2,1)S(1)}, bf16[1024,128]{1,0:T(8,128)(2,1)}, u32[]{:S(2)}) copy-start(bf16[1024,128]{1,0:T(8,128)(2,1)} %param.27) | copy-start | bytes 786436
  7.2 1.9 copy-start.1
  7.2 2.7 %copy-start.9 = (f32[256]{0:T(256)S(1)}, f32[256]{0:T(256)}, u32[]{:S(2)}) copy-start(f32[256]{0:T(256)} %param.18) | copy-start | bytes 3076
  10.5 10.7 %copy-start.8 = (s32[512]{0:T(512)S(1)}, s32[512]{0:T(512)}, u32[]{:S(2)}) copy-start(s32[512]{0:T(512)} %param.16) | copy-start | bytes 6148
  15.7 17.1 %all-to-all-start = ((bf16[8,64,1,3,256]{4,1,3,2,0:T(8,128)(2,1)}), bf16[8,64,1,3,256]{4,1,3,2,0:T(8,128)(2,1)S(1)}, u32[]{:S(2)}, u32[]{:S(2)}) async-start(bf16[8,64,1,3,256]{4,1,3,2,0:T(8,128)(2,1)} %fusion.16), calls=%async_computation | async-start | bytes 1572864 | tf_op jit(solution)/shard_map/all_to_all | solution.py:13
  21.3 15.6 %copy-start.5 = (bf16[256,256]{1,0:T(8,128)(2,1)S(1)}, bf16[256,256]{1,0:T(8,128)(2,1)}, u32[]{:S(2)}) copy-start(bf16[256,256]{1,0:T(8,128)(2,1)} %param.22) | copy-start | bytes 393220
  38.1 5.6 %copy-start.6 = (bf16[256,256]{1,0:T(8,128)(2,1)S(1)}, bf16[256,256]{1,0:T(8,128)(2,1)}, u32[]{:S(2)}) copy-start(bf16[256,256]{1,0:T(8,128)(2,1)} %param.20) | copy-start | bytes 393220
  45.0 5.6 %copy-start.7 = (bf16[256,256]{1,0:T(8,128)(2,1)S(1)}, bf16[256,256]{1,0:T(8,128)(2,1)}, u32[]{:S(2)}) copy-start(bf16[256,256]{1,0:T(8,128)(2,1)} %param.21) | copy-start | bytes 393220
  55.1 2.4 copy-start.3
  101.6 19.2 %all-to-all-start.1 = ((bf16[512,1,3,256]{3,2,1,0:T(4,128)(2,1)}), bf16[512,1,3,256]{3,2,1,0:T(4,128)(2,1)S(1)}, u32[]{:S(2)}, u32[]{:S(2)}) async-start(bf16[512,1,3,256]{3,2,1,0:T(4,128)(2,1)} %bitcast.129), calls=%async_computation.1 | async-start | bytes 2097152 | tf_op jit(solution)/shard_map/all_to_all | solution.py:101
  105.9 101.0 %all-gather.2.cloned.1.call-start = ((), (), s32[]{:S(2)}) async-start(), calls=%async_computation.5 | async-start | bytes 3244032 | tf_op jit(solution)/shard_map/all_gather | solution.py:149
  120.8 0.9 copy-start.4
  122.6 30.4 %copy-start.2 = (f32[64,24,256]{2,1,0:T(8,128)}, f32[64,24,256]{2,1,0:T(8,128)S(1)}, u32[]{:S(2)}) copy-start(f32[64,24,256]{2,1,0:T(8,128)S(1)} %get-tuple-element.100) | copy-start | bytes 4718596
  122.6 0.9 copy-start.10
  122.6 0.9 copy-start.12
  123.4 29.6 %copy-start.11 = (bf16[256,32]{0,1:T(8,128)(2,1)S(1)}, bf16[256,32]{0,1:T(8,128)(2,1)}, u32[]{:S(2)}) copy-start(bf16[256,32]{0,1:T(8,128)(2,1)} %param.26) | copy-start | bytes 49156
  155.2 13.7 %all-to-all-start.4 = ((bf16[8,64,768]{2,1,0:T(8,128)(2,1)}), bf16[8,64,768]{2,1,0:T(8,128)(2,1)S(1)}, u32[]{:S(2)}, u32[]{:S(2)}) async-start(bf16[8,64,768]{2,1,0:T(8,128)(2,1)} %broadcast_in_dim.23), calls=%async_computation.4 | async-start | bytes 1572864 | tf_op jit(solution)/shard_map/all_to_all | solution.py:21
Sparse Core Ops, SparseCore 0:
  153.1 53.7 all-gather.1
